TPU v7x, 32 devices: a whole 2x2x4 slice. The times are simulated.
32 devices in a mesh: dom: 16 (over z, y, core), sub: 2 (over x).
Axes of the slice: x: 2, y: 2, z: 4, core: 2. Of those that a mesh axis runs over, the one named last changes fastest.
Arguments:
- fine_partial: float32 [2, 165, 2048], P('sub', None, 'dom'), may hold values from -6 to 6
- upward_ops: float32 [8, 165, 165], replicated, may hold values from -0.15625 to 0.15625
- interaction_ops: float32 [188, 165, 165], P('sub'), may hold values from -0.03125 to 0.03125
- downward_ops: float32 [8, 165, 165], replicated, may hold values from -0.5 to 0.5
- fine_list: int32 [188, 2048], P('sub', 'dom'), may hold values from -1 to 2047, as said below
- mid_list: int32 [188, 256], P('sub', 'dom'), may hold values from -1 to 255, as said below
- top_list: int32 [188, 32], P('sub', 'dom'), may hold values from -1 to 31, as said below
- upper_list: int32 [188, 4], P('sub'), may hold values from -1 to 3, as said below
- positions: float32 [3, 65536], P(None, ('dom', 'sub')), may hold values from -0.5 to 0.5
- leaf_cell: int32 [65536], P(('dom', 'sub')), may hold values from 0 to 2047, as said below
Outputs:
- local_fine: float32 [165, 2048], P(None, 'dom')
- potential: float32 [65536], P(('dom', 'sub'))
Inputs may be any that keep to these rules, and one draw needn't show every extreme that they name: `fine_list`: column t lists for each offset slot a cell of the finest level within 128 cells of t in Peano order, or -1 for an empty slot. `mid_list`: column t lists for each offset slot a cell of the middle level within 16 cells of t, or -1 for an empty slot. `top_list`: each entry is a cell of the top level, or -1 for an empty slot. `upper_list`: each entry is a cell of the upper level, or -1 for an empty slot. `leaf_cell`: A particle's leaf is one of the 128 finest cells owned by its own slab.
All inputs are finite; a program needn't handle non-finite values.
Results may differ from a plain program's by a relative error of at most 0.0003.
Values sent between devices are 32-bit elements; how exact they have to be, the bound alone decides.
A program may use at most 128 MiB of HBM per device.

v0:
```python
import functools

import jax
import jax.numpy as jnp
from jax import lax
from jax.experimental import pallas as pl
from jax.experimental.pallas import tpu as pltpu
from jax.sharding import PartitionSpec as P

ORDER = 8
LANES = 128


precise = lax.Precision.HIGHEST


def round_up(count, unit):
    return -(-count // unit) * unit


def exponents():
    entries = []
    for degree in range(ORDER + 1):
        for along_x in range(degree, -1, -1):
            for along_y in range(degree - along_x, -1, -1):
                entries.append((along_x, along_y, degree - along_x - along_y))
    return entries


def halves(value):
    high = value.astype(jnp.bfloat16)
    low = (value - high.astype(jnp.float32)).astype(jnp.bfloat16)
    return high, low


def one_hot(row, count):
    places = lax.broadcasted_iota(jnp.int32, (count, row.shape[1]), 0)
    return jnp.where(places == row, 1.0, 0.0).astype(jnp.bfloat16)


def interact_kernel(
    coeffs, slots, group, spread, tops, fine_ref, tops_ref, upward_ref, fine_list, coarse_list,
    ops_ref, out_ref,
    fine_table, coarse_table, fine_picked, coarse_picked, held,
):
    rows = fine_ref.shape[0]
    depth = fine_list.shape[0]
    step = pl.program_id(0)

    @pl.when(step == 0)
    def _():
        ops_high, ops_low = split_upward(upward_ref, held)
        width = coarse_table.shape[1]

        def shifted(value, amount):
            extra = width - value.shape[1]
            if extra:
                filler = jnp.zeros((rows, extra), jnp.float32)
                value = jnp.concatenate([value, filler], axis=1)
            return pltpu.roll(value, amount, 1) if amount else value

        top_moments = jnp.transpose(tops_ref[...])[:rows]
        coarse = shifted(raise_level(fine_ref[...], ops_high, ops_low), 0)
        coarse += shifted(top_moments, spread)
        coarse += shifted(raise_level(top_moments, ops_high, ops_low), spread + tops)
        for source, table in ((fine_ref[...], fine_table), (coarse, coarse_table)):
            high, low = halves(source)
            table[...] = jnp.concatenate([high, low], axis=0)

        def pick(batch, carry):
            base = pl.multiple_of(8 * batch, 8)
            for table, entries, picked in (
                (fine_table, fine_list, fine_picked),
                (coarse_table, coarse_list, coarse_picked),
            ):
                columns = []
                for k in range(0, 8, 2):
                    chosen = jnp.concatenate(
                        [
                            one_hot(entries[pl.ds(base + k + m, 1), :], table.shape[1])
                            for m in range(2)
                        ],
                        axis=1,
                    )
                    both = jnp.dot(table[...], chosen, preferred_element_type=jnp.float32)
                    value = both[:rows] + both[rows:]
                    columns += [value[:, :LANES], value[:, LANES:]]
                picked[:, pl.ds(base, 8), :] = jnp.swapaxes(jnp.stack(columns), 0, 1)
            return carry

        lax.fori_loop(0, depth // 8, pick, 0)
        out_ref[...] = jnp.zeros_like(out_ref)

    lane = lax.broadcasted_iota(jnp.int32, (rows, LANES), 1)
    filler = jnp.zeros((LANES - depth, 2 * LANES), jnp.bfloat16)
    for part in range(group // 8):
        block = jnp.swapaxes(ops_ref[:, 8 * part : 8 * part + 8, :], 0, 1)
        left = []
        right = []
        for k in range(8):
            term = step * group + 8 * part + k
            op = jnp.where((lane < slots) & (term < coeffs), block[k], 0.0)
            op_high, op_low = halves(op)
            data = jnp.concatenate([fine_picked[term], coarse_picked[term]], axis=1)
            high, low = halves(data)
            high = jnp.concatenate([high, filler], axis=0)
            low = jnp.concatenate([low, filler], axis=0)
            left += [op_high, op_high, op_low]
            right += [high, low, high]
        out_ref[...] += jnp.dot(
            jnp.concatenate(left, axis=1),
            jnp.concatenate(right, axis=0),
            preferred_element_type=jnp.float32,
        )


def interact(fine, tops_rows, upward_ops, fine_list, coarse_list, ops, spread, tops, coarse_width):
    coeffs, _, slots = ops.shape
    rows, width = fine.shape
    depth = fine_list.shape[0]
    group = 24
    whole = lambda array: pl.BlockSpec(array.shape, lambda i: (0, 0))
    return pl.pallas_call(
        functools.partial(interact_kernel, coeffs, slots, group, spread, tops),
        grid=(rows // group,),
        in_specs=[
            whole(fine),
            whole(tops_rows),
            pl.BlockSpec((coeffs, 8, coeffs), lambda i: (0, 0, 0)),
            whole(fine_list),
            whole(coarse_list),
            pl.BlockSpec((rows, group, LANES), lambda i: (0, i, 0)),
        ],
        out_specs=pl.BlockSpec((rows, 2 * LANES), lambda i: (0, 0)),
        out_shape=jax.ShapeDtypeStruct((rows, 2 * LANES), jnp.float32),
        scratch_shapes=[
            pltpu.VMEM((2 * rows, width), jnp.bfloat16),
            pltpu.VMEM((2 * rows, coarse_width), jnp.bfloat16),
            pltpu.VMEM((rows, depth, LANES), jnp.float32),
            pltpu.VMEM((rows, depth, LANES), jnp.float32),
            pltpu.VMEM((rows, 8, 2 * LANES), jnp.float32),
        ],
        compiler_params=pltpu.CompilerParams(vmem_limit_bytes=48 * 1024 * 1024),
        cost_estimate=pl.CostEstimate(
            flops=6 * rows * rows * LANES * 2 * LANES,
            bytes_accessed=4 * rows * rows * LANES,
            transcendentals=0,
        ),
    )(fine, tops_rows, jnp.transpose(upward_ops, (1, 0, 2)), fine_list, coarse_list, ops)


def potential_kernel(local_ref, leaf_ref, position_ref, exponent_ref, out_ref):
    rows, cells = local_ref.shape
    particles = leaf_ref.shape[1]
    high, low = halves(local_ref[...])
    table = jnp.concatenate([high, low], axis=0)
    masks = [
        [(exponent_ref[:, axis : axis + 1] // bit) % 2 == 1 for bit in (1, 2, 4, 8)]
        for axis in range(3)
    ]
    for start in range(0, particles, 2 * LANES):
        span = slice(start, start + 2 * LANES)
        chosen = one_hot(leaf_ref[:, span], cells)
        both = jnp.dot(table, chosen, preferred_element_type=jnp.float32)
        value = both[:rows] + both[rows:]
        for axis in range(3):
            power = position_ref[axis : axis + 1, span]
            for bit in range(4):
                value = value * jnp.where(masks[axis][bit], power, 1.0)
                power = power * power
        out_ref[:, span] = jnp.sum(value, axis=0, keepdims=True)


def evaluate(local, leaves, positions):
    rows = local.shape[0]
    table = jnp.asarray(exponents(), jnp.int32)
    table = jnp.pad(table, ((0, rows - table.shape[0]), (0, LANES - 3)))
    return pl.pallas_call(
        potential_kernel,
        out_shape=jax.ShapeDtypeStruct((1, leaves.shape[0]), jnp.float32),
        compiler_params=pltpu.CompilerParams(vmem_limit_bytes=32 * 1024 * 1024),
    )(local, leaves[None], positions, table)[0]


def raise_level(moments, ops_high, ops_low):
    rows, width = moments.shape
    parents = round_up(width // 8, LANES)
    high, low = halves(moments)
    source = lax.broadcasted_iota(jnp.int32, (width, 8 * parents), 0)
    target = lax.broadcasted_iota(jnp.int32, (width, 8 * parents), 1)
    wanted = 8 * (target % parents) + target // parents
    chosen = jnp.where(source == wanted, 1.0, 0.0).astype(jnp.bfloat16)
    both = jnp.dot(
        jnp.concatenate([high, low], axis=0), chosen, preferred_element_type=jnp.float32
    )
    filler = jnp.zeros((2 * LANES - rows, parents), jnp.float32)
    stacks = []
    for first in (0, rows):
        pieces = []
        for o in range(8):
            pieces += [both[first : first + rows, o * parents : (o + 1) * parents], filler]
        stacks.append(jnp.concatenate(pieces, axis=0).astype(jnp.bfloat16))
    dot = functools.partial(jnp.dot, preferred_element_type=jnp.float32)
    return dot(ops_high, stacks[0]) + dot(ops_high, stacks[1]) + dot(ops_low, stacks[0])


def split_upward(upward_ref, held):
    coeffs = upward_ref.shape[0]
    held[...] = jnp.zeros_like(held)
    held[:coeffs, :, :coeffs] = upward_ref[...]
    ops = jnp.swapaxes(held[...], 0, 1)
    return halves(jnp.concatenate([ops[o] for o in range(8)], axis=1))


def prepare(
    counts, partial_ref, upward_ref, fine_ref, mid_ref, top_ref, upper_ref,
    rows_out, fine_out, coarse_out, held, lists,
):
    rows = held.shape[0]
    coeffs = partial_ref.shape[0]
    slots = fine_ref.shape[0]
    slab, mid, top, spread, tops = counts
    domain = lax.axis_index("dom")
    filler = jnp.zeros((rows - coeffs, partial_ref.shape[1]), jnp.float32)
    block = jnp.concatenate([partial_ref[...], filler], axis=0)
    high, low = split_upward(upward_ref, held)
    top_moments = raise_level(raise_level(block, high, low), high, low)
    filler = jnp.zeros((2 * LANES - rows, LANES), jnp.float32)
    turned = jnp.transpose(jnp.concatenate([top_moments, filler], axis=0))
    rows_out[...] = turned[: rows_out.shape[0]]

    def place(sources, offset):
        return jnp.where(sources >= 0, sources + offset, -1)

    fine_out[...] = jnp.full_like(fine_out, -1)
    fine_out[:slots, :] = place(fine_ref[...], slab - domain * slab)
    lists[...] = jnp.full_like(lists, -1.0)
    start = 0
    for part in (
        place(mid_ref[...], mid - domain * mid),
        place(top_ref[...], spread),
        place(upper_ref[pl.ds(domain * top // 8, 1), :], spread + tops),
    ):
        lists[start : start + part.shape[0], :slots] = part.astype(jnp.float32)
        start += part.shape[0]
    coarse = jnp.transpose(lists[...])
    coarse_out[...] = coarse[: coarse_out.shape[0]].astype(jnp.int32)


def exchange_kernel(
    domains, subs, counts, block_ref, partial_ref, upward_ref, fine_ref, mid_ref, top_list_ref,
    upper_ref, wide_out, tops_out, fine_out, coarse_out,
    low, high, tops, top_ref, held, lists, side_send, side_recv, top_send, top_recv,
):
    domain, sub = lax.axis_index("dom"), lax.axis_index("sub")
    count = domains * subs
    flat = domain * subs + sub
    mesh = pl.DeviceIdType.MESH
    coeffs, cells = block_ref.shape
    top_cells = top_ref.shape[0]

    def peer(offset):
        place = lax.rem(flat + offset, count)
        return {"dom": place // subs, "sub": lax.rem(place, subs)}

    barrier = pltpu.get_barrier_semaphore()

    def greet(offset, carry):
        pl.semaphore_signal(barrier, inc=1, device_id=peer(offset), device_id_type=mesh)
        return carry

    lax.fori_loop(1, count, greet, 0)
    prepare(
        counts, partial_ref, upward_ref, fine_ref, mid_ref, top_list_ref, upper_ref,
        top_ref, fine_out, coarse_out, held, lists,
    )
    tops[count - 1] = top_ref[...]
    tops_out[...] = jnp.zeros_like(tops_out)
    wide_out[...] = jnp.zeros_like(wide_out)
    wide_out[:coeffs, cells : 2 * cells] = block_ref[...]
    pl.semaphore_wait(barrier, count - 1)

    def send(offset, carry):
        pltpu.make_async_remote_copy(
            src_ref=top_ref,
            dst_ref=tops.at[offset - 1],
            send_sem=top_send,
            recv_sem=top_recv,
            device_id=peer(offset),
            device_id_type=mesh,
        ).start()
        return carry

    lax.fori_loop(1, count, send, 0)
    copies = []
    for index, (target, move) in enumerate(((low, 1), (high, domains - 1))):
        side = pltpu.make_async_remote_copy(
            src_ref=block_ref,
            dst_ref=target,
            send_sem=side_send.at[index],
            recv_sem=side_recv.at[index],
            device_id={"dom": lax.rem(domain + move, domains), "sub": sub},
            device_id_type=mesh,
        )
        side.start()
        copies.append(side)
    arrived = tops.at[pl.ds(0, count - 1)]
    pltpu.make_async_copy(arrived, arrived, top_recv).wait()

    def gather(offset, carry):
        source = lax.rem(flat + count - offset, count) // subs
        slot = lax.rem(offset + count - 1, count)
        for r in range(top_cells):
            at = pl.ds(source * top_cells + r, 1)
            tops_out[at, :] = tops_out[at, :] + tops[slot, r : r + 1, :]
        return carry

    lax.fori_loop(0, count, gather, 0)
    for side in copies:
        side.wait()
    wide_out[:coeffs, :cells] = low[...]
    wide_out[:coeffs, 2 * cells :] = high[...]
    pltpu.make_async_copy(arrived, arrived, top_send).wait()


def exchange(block, partial, upward_ops, fine_list, mid_list, top_list, upper_list, rows, depth, counts):
    domains, subs = lax.axis_size("dom"), lax.axis_size("sub")
    coeffs, cells = block.shape
    top_cells = top_list.shape[1]
    vmem = pl.BlockSpec(memory_space=pltpu.VMEM)
    return pl.pallas_call(
        functools.partial(exchange_kernel, domains, subs, counts),
        in_specs=[vmem] * 7,
        out_specs=[vmem] * 4,
        out_shape=[
            jax.ShapeDtypeStruct((rows, 3 * cells), jnp.float32),
            jax.ShapeDtypeStruct((round_up(counts[4], LANES), 2 * LANES), jnp.float32),
            jax.ShapeDtypeStruct((depth, LANES), jnp.int32),
            jax.ShapeDtypeStruct((depth, LANES), jnp.int32),
        ],
        scratch_shapes=[
            pltpu.VMEM(block.shape, jnp.float32),
            pltpu.VMEM(block.shape, jnp.float32),
            pltpu.VMEM((domains * subs, top_cells, 2 * LANES), jnp.float32),
            pltpu.VMEM((top_cells, 2 * LANES), jnp.float32),
            pltpu.VMEM((rows, 8, 2 * LANES), jnp.float32),
            pltpu.VMEM((LANES, LANES), jnp.float32),
            pltpu.SemaphoreType.DMA((2,)),
            pltpu.SemaphoreType.DMA((2,)),
            pltpu.SemaphoreType.DMA,
            pltpu.SemaphoreType.DMA,
        ],
        compiler_params=pltpu.CompilerParams(
            collective_id=0, has_side_effects=True, vmem_limit_bytes=32 * 1024 * 1024
        ),
    )(
        block,
        partial,
        jnp.transpose(upward_ops, (1, 0, 2)),
        fine_list,
        jnp.transpose(mid_list),
        jnp.transpose(top_list),
        jnp.transpose(upper_list),
    )


def downward(expansions, downward_ops):
    spread = jnp.einsum("oab,bp->apo", downward_ops, expansions, precision=precise)
    return spread.reshape(spread.shape[0], -1)


def settle(portion):
    count = lax.axis_size("sub")
    ring = [(i, (i + 1) % count) for i in range(count)]
    total = moving = portion
    for _ in range(count - 1):
        moving = lax.ppermute(moving, "sub", ring)
        total = total + moving
    return total


def shards(
    fine_partial,
    upward_ops,
    interaction_ops,
    downward_ops,
    fine_list,
    mid_list,
    top_list,
    upper_list,
    positions,
    leaf_cell,
):
    slab_cells = fine_partial.shape[2]
    mid_cells = slab_cells // 8
    top_cells = slab_cells // 64
    domain = lax.axis_index("dom")
    slots, coeffs = interaction_ops.shape[:2]
    rows = round_up(coeffs, 24)
    depth = round_up(slots, 16)
    upper_span = max(1, top_cells // 8)
    spread = 3 * mid_cells
    tops = top_cells * lax.axis_size("dom")
    coarse_width = round_up(spread + tops + tops // 8, LANES)
    counts = (slab_cells, mid_cells, top_cells, spread, tops)
    partial = fine_partial[0]
    wide_fine, top_moments, fine_sources, coarse_sources = exchange(
        settle(partial), partial, upward_ops, fine_list, mid_list, top_list, upper_list,
        rows, depth, counts,
    )

    def padded(array, height, width, fill):
        return jnp.pad(
            array,
            ((0, height - array.shape[0]), (0, width - array.shape[1])),
            constant_values=fill,
        )

    terms = interact(
        wide_fine, top_moments, upward_ops, fine_sources, coarse_sources,
        jnp.transpose(interaction_ops, (1, 2, 0)), spread, tops, coarse_width,
    )
    terms = settle(terms)[:coeffs]
    at = LANES
    mid_term = terms[:, at : at + mid_cells]
    at += mid_cells
    top_term = terms[:, at : at + top_cells]
    at += top_cells
    local_upper = terms[:, at : at + upper_span]
    down_top = downward(local_upper, downward_ops)
    top_offset = domain * top_cells % 8
    local_top = top_term + lax.dynamic_slice_in_dim(down_top, top_offset, top_cells, 1)
    local_mid = mid_term + downward(local_top, downward_ops)
    local_fine = terms[:, :slab_cells] + downward(local_mid, downward_ops)
    potential = evaluate(
        padded(local_fine, rows, slab_cells, 0), leaf_cell - domain * slab_cells, positions
    )
    return (local_fine, potential)


def solution(mesh):
    placed = (
        P("sub", None, "dom"),
        P(),
        P("sub", None, None),
        P(),
        P("sub", "dom"),
        P("sub", "dom"),
        P("sub", "dom"),
        P("sub", None),
        P(None, ("dom", "sub")),
        P(("dom", "sub")),
    )
    return jax.shard_map(
        shards,
        mesh=mesh,
        in_specs=placed,
        out_specs=(P(None, "dom"), P(("dom", "sub"))),
        check_vma=False,
    )
```

profile of v0, /device:TPU:0, one launch (start us, length us, event | category | flops | bytes accessed | tf_op | source)
XLA Modules:
  0.0 61.7 jit_solution(17702831554189748802)
XLA Ops:
  0.6 0.9 %copy.58 = f32[1,165,128]{2,1,0:T(8,128)S(1)} copy(f32[1,165,128]{2,0,1:T(1,128)} %param.11) | data formatting | bytes 168960
  1.5 3.0 %collective-permute-start = (f32[165,128]{1,0:T(8,128)S(1)}, f32[165,128]{1,0:T(8,128)S(1)}, u32[]{:S(2)}, u32[]{:S(2)}) collective-permute-start(f32[165,128]{1,0:T(8,128)S(1)} %bitcast.41), channel_id=1, source_target_pairs={{0,1},{1,0},{2,3},{3,2},{4,5},{5,4},{6,7},{7,6},{8,9},{9,8},{10,11... | collective-permute-start | bytes 253448 | tf_op jit(solution)/shard_map/ppermute | solution.py:377
  4.5 2.5 %collective-permute-done = f32[165,128]{1,0:T(8,128)S(1)} collective-permute-done((f32[165,128]{1,0:T(8,128)S(1)}, f32[165,128]{1,0:T(8,128)S(1)}, u32[]{:S(2)}, u32[]{:S(2)}) %collective-permute-start) | collective-permute-done | bytes 84512 | tf_op jit(solution)/shard_map/ppermute | solution.py:377
  7.0 0.9 %fusion.17.block_ref = f32[165,128]{1,0:T(8,128)S(1)} fusion(f32[165,128]{1,0:T(8,128)S(1)} %collective-permute-done, f32[1,165,128]{2,0,1:T(1,128)} %param.11), kind=kLoop, calls=%fused_computation.20 | loop fusion | flops 21120 | bytes 253440 | tf_op jit(solution)/shard_map/add | solution.py:378
  7.9 0.0 copy-start
  7.9 1.3 %copy-done = f32[8,165,165]{2,0,1:T(8,128)S(1)} copy-done((f32[8,165,165]{2,0,1:T(8,128)S(1)}, f32[8,165,165]{2,0,1:T(8,128)}, u32[]{:S(2)}) %copy-start) | copy-done | bytes 871224
  9.3 0.0 copy-start.3
  9.3 0.8 %copy-done.3 = s32[94,128]{1,0:T(8,128)S(1)} copy-done((s32[94,128]{1,0:T(8,128)S(1)}, s32[94,128]{1,0:T(8,128)}, u32[]{:S(2)}) %copy-start.3) | copy-done | bytes 48152
  10.1 0.0 copy-start.5
  10.1 0.7 %copy-done.5 = s32[94,16]{0,1:T(8,128)S(1)} copy-done((s32[94,16]{0,1:T(8,128)S(1)}, s32[94,16]{0,1:T(8,128)}, u32[]{:S(2)}) %copy-start.5) | copy-done | bytes 6040
  10.8 0.0 copy-start.6
  10.8 0.7 %copy-done.6 = s32[94,4]{0,1:T(4,128)S(1)} copy-done((s32[94,4]{0,1:T(4,128)S(1)}, s32[94,4]{0,1:T(4,128)}, u32[]{:S(2)}) %copy-start.6) | copy-done | bytes 1528
  11.4 0.0 copy-start.7
  11.4 0.7 %copy-done.7 = s32[94,2]{0,1:T(2,128)S(1)} copy-done((s32[94,2]{0,1:T(2,128)S(1)}, s32[94,2]{0,1:T(2,128)}, u32[]{:S(2)}) %copy-start.7) | copy-done | bytes 776
  12.1 0.0 copy-start.1
  12.1 12.1 %shard_map.122 = (f32[168,384]{1,0:T(8,128)S(1)}, f32[128,256]{1,0:T(8,128)S(1)}, s32[96,128]{1,0:T(8,128)S(1)}, s32[96,128]{1,0:T(8,128)S(1)}) custom-call(f32[165,128]{1,0:T(8,128)S(1)} %fusion.17.block_ref, f32[165,128]{1,0:T(8,128)S(1)} %bitcast.42, f32[165,8,165]{2,1,0:T(8,128)S(1)} %bitcast.39, s32[94,128]{1,0:T(8,128)S(1)} %copy-done.3, ...), custom_call_target="tpu_custom_call" | custom-call | tf_op jit(solution)/shard_map/pallas_call | solution.py:331
  24.2 0.0 copy-done.1
  24.2 0.0 copy-start.10
  24.2 0.0 copy-start.8
  24.3 24.3 %shard_map.123 = f32[168,256]{1,0:T(8,128)S(1)} custom-call(f32[168,384]{1,0:T(8,128)S(1)} %get-tuple-element.6.fine_ref, f32[128,256]{1,0:T(8,128)S(1)} %get-tuple-element.7.tops_ref, f32[165,8,165]{2,1,0:T(8,128)S(1)} %bitcast.40, s32[96,128]{1,0:T(8,128)S(1)} %get-tuple-element.8.fine_list, s32[96,128]{1,0:T(8,128)S(1)} %get-tuple-element.9.coarse_list, ...), custom_call_target="tpu_custom_call" | custom-call | flops 5549064192 | bytes 14450688 | tf_op jit(solution)/shard_map/pallas_call | solution.py:123
  48.5 0.7 %collective-permute-start.1 = (f32[168,256]{1,0:T(8,128)S(1)}, f32[168,256]{1,0:T(8,128)S(1)}, u32[]{:S(2)}, u32[]{:S(2)}) collective-permute-start(f32[168,256]{1,0:T(8,128)S(1)} %shard_map.123), channel_id=1, source_target_pairs={{0,1},{1,0},{2,3},{3,2},{4,5},{5,4},{6,7},{7,6},{8,9},{9,8},{10,11... | collective-permute-start | bytes 516104 | tf_op jit(solution)/shard_map/ppermute | solution.py:377
  49.2 0.0 copy-done.10
  49.2 5.8 %collective-permute-done.1 = f32[168,256]{1,0:T(8,128)S(1)} collective-permute-done((f32[168,256]{1,0:T(8,128)S(1)}, f32[168,256]{1,0:T(8,128)S(1)}, u32[]{:S(2)}, u32[]{:S(2)}) %collective-permute-start.1) | collective-permute-done | bytes 172064 | tf_op jit(solution)/shard_map/ppermute | solution.py:377
  55.0 0.2 slice_reduce_fusion
  55.2 0.0 copy-done.8
  55.2 0.3 multiply_reduce_fusion
  55.5 1.7 %fusion.7 = f32[165,2,8]{0,1,2:T(2,128)S(1)} fusion(f32[8,165,165]{2,0,1:T(8,128)S(1)} %copy-done.8, f32[168,256]{1,0:T(8,128)S(1)} %add.27, f32[8,165]{0,1:T(8,128)S(1)} %multiply_reduce_fusion, s32[]{:T(128)S(6)} %select_n.11), kind=kOutput, calls=%fused_computation.6 | convolution fusion | flops 5227530 | bytes 1534276 | tf_op jit(solution)/shard_map/oab,bp->apo/dot_general | solution.py:368
  57.1 0.0 copy-start.2
  57.2 0.0 copy-start.4
  57.2 0.1 copy.30
  57.3 1.6 %fusion.4 = f32[165,16,8]{0,1,2:T(8,128)S(1)} fusion(f32[8,165,165]{2,0,1:T(8,128)S(1)} %copy-done.8, f32[165,16]{1,0:T(8,128)S(1)} %copy.30, f32[168,256]{1,0:T(8,128)S(1)} %add.27), kind=kOutput, calls=%fused_computation.5 | convolution fusion | flops 41820240 | bytes 1608192 | tf_op jit(solution)/shard_map/oab,bp->apo/dot_general | solution.py:368
  58.9 0.1 copy.57
  59.0 0.1 copy.34
  59.1 0.0 copy-start.9
  59.1 0.0 copy-done.2
  59.1 0.0 copy-done.4
  59.1 2.5 %shard_map.124 = f32[1,2048]{1,0:T(1,128)} custom-call(f32[168,128]{1,0:T(8,128)S(1)} %pad.8.local_ref, s32[1,2048]{1,0:T(1,128)S(1)} %bitcast.43, f32[3,2048]{1,0:T(4,128)S(1)} %copy-done.4, s32[168,128]{1,0:T(8,128)S(1)} %copy-done.2), custom_call_target="tpu_custom_call" | custom-call | tf_op jit(solution)/shard_map/pallas_call | solution.py:178
  61.7 0.0 copy-done.9
  (5 shorter events, 0.1 us)
Async XLA Ops:
  1.5 5.5 %collective-permute-start = (f32[165,128]{1,0:T(8,128)S(1)}, f32[165,128]{1,0:T(8,128)S(1)}, u32[]{:S(2)}, u32[]{:S(2)}) collective-permute-start(f32[165,128]{1,0:T(8,128)S(1)} %bitcast.41), channel_id=1, source_target_pairs={{0,1},{1,0},{2,3},{3,2},{4,5},{5,4},{6,7},{7,6},{8,9},{9,8},{10,11... | collective-permute-start | bytes 253448 | tf_op jit(solution)/shard_map/ppermute | solution.py:377
  7.9 1.3 %copy-start = (f32[8,165,165]{2,0,1:T(8,128)S(1)}, f32[8,165,165]{2,0,1:T(8,128)}, u32[]{:S(2)}) copy-start(f32[8,165,165]{2,0,1:T(8,128)} %param.12) | copy-start | bytes 2613604
  9.3 0.8 %copy-start.3 = (s32[94,128]{1,0:T(8,128)S(1)}, s32[94,128]{1,0:T(8,128)}, u32[]{:S(2)}) copy-start(s32[94,128]{1,0:T(8,128)} %fine_ref.1) | copy-start | bytes 144388
  10.1 0.7 %copy-start.5 = (s32[94,16]{0,1:T(8,128)S(1)}, s32[94,16]{0,1:T(8,128)}, u32[]{:S(2)}) copy-start(s32[94,16]{0,1:T(8,128)} %param.16) | copy-start | bytes 18052
  10.8 0.7 %copy-start.6 = (s32[94,4]{0,1:T(4,128)S(1)}, s32[94,4]{0,1:T(4,128)}, u32[]{:S(2)}) copy-start(s32[94,4]{0,1:T(4,128)} %param.18) | copy-start | bytes 4516
  11.4 0.7 %copy-start.7 = (s32[94,2]{0,1:T(2,128)S(1)}, s32[94,2]{0,1:T(2,128)}, u32[]{:S(2)}) copy-start(s32[94,2]{0,1:T(2,128)} %param.17) | copy-start | bytes 2260
  12.1 12.1 %copy-start.1 = (f32[8,165,165]{2,0,1:T(8,128)S(1)}, f32[8,165,165]{2,0,1:T(8,128)}, u32[]{:S(2)}) copy-start(f32[8,165,165]{2,0,1:T(8,128)} %param.12) | copy-start | bytes 2613604
  24.2 25.0 %copy-start.10 = (s32[2048]{0:T(1024)S(1)}, s32[2048]{0:T(1024)}, u32[]{:S(2)}) copy-start(s32[2048]{0:T(1024)} %param.20) | copy-start | bytes 24580
  24.2 31.0 %copy-start.8 = (f32[8,165,165]{2,0,1:T(8,128)S(1)}, f32[8,165,165]{2,0,1:T(8,128)}, u32[]{:S(2)}) copy-start(f32[8,165,165]{2,0,1:T(8,128)} %param.14) | copy-start | bytes 2613604
  48.5 6.5 %collective-permute-start.1 = (f32[168,256]{1,0:T(8,128)S(1)}, f32[168,256]{1,0:T(8,128)S(1)}, u32[]{:S(2)}, u32[]{:S(2)}) collective-permute-start(f32[168,256]{1,0:T(8,128)S(1)} %shard_map.123), channel_id=1, source_target_pairs={{0,1},{1,0},{2,3},{3,2},{4,5},{5,4},{6,7},{7,6},{8,9},{9,8},{10,11... | collective-permute-start | bytes 516104 | tf_op jit(solution)/shard_map/ppermute | solution.py:377
  57.1 2.0 %copy-start.2 = (s32[168,128]{1,0:T(8,128)S(1)}, s32[168,128]{1,0:T(8,128)}, u32[]{:S(2)}) copy-start(s32[168,128]{1,0:T(8,128)} %constant.36.exponent_ref) | copy-start | bytes 258052
  57.2 2.0 %copy-start.4 = (f32[3,2048]{1,0:T(4,128)S(1)}, f32[3,2048]{1,0:T(4,128)}, u32[]{:S(2)}) copy-start(f32[3,2048]{1,0:T(4,128)} %position_ref.1) | copy-start | bytes 73732
  59.1 2.6 %copy-start.9 = (f32[165,128]{1,0:T(8,128)}, f32[165,128]{1,0:T(8,128)S(1)}, u32[]{:S(2)}) copy-start(f32[165,128]{1,0:T(8,128)S(1)} %slice_add_fusion.2) | copy-start | bytes 253444
where the time goes:
time: 62.2 us; the launch traced here: 61.7 us
  Pallas kernels  38.9 us (63%)
  waiting for transfers between devices  8.31 us (13%)
  local copies, waits for them, and re-layouts  5.58 us (9%)
  starting transfers between devices  3.64 us (6%)
  matrix products  3.26 us (5%)
  other arithmetic  1.19 us (2%)
  between operations  0.78 us (1%)
    pallas_call x1, Pallas kernels, interact(): pl.pallas_call(functools.partial(interact_kernel, coeffs, slots, group, s...  24.3 us
    pallas_call x1, Pallas kernels, exchange(): pl.pallas_call(functools.partial(exchange_kernel, domains, subs, counts),...  12.1 us
    ppermute x2, waiting for transfers between devices, settle(): moving = lax.ppermute(moving, 'sub', ring)  8.31 us
    unnamed x23, local copies, waits for them, and re-layouts  5.11 us
    ppermute x2, starting transfers between devices, settle(): moving = lax.ppermute(moving, 'sub', ring)  3.64 us
    dot_general x2, matrix products, downward(): jnp.einsum('oab,bp->apo', downward_ops, expansions, precision=precise)  3.26 us
    pallas_call x1, Pallas kernels, evaluate(): pl.pallas_call(potential_kernel, out_shape=jax.ShapeDtypeStruct((1, leave...  2.54 us
  transfers between devices with their start and end apart: 2, of which 2 were waited for; matrix products, arithmetic and copies ran while one was open for 0% of the time, Pallas kernels for 0%

commit v1 on v0

--- a/solution.py
+++ b/solution.py
@@ -38,109 +38,130 @@
     return jnp.where(places == row, 1.0, 0.0).astype(jnp.bfloat16)
 
 
+def matmul(left, right):
+    return jnp.dot(left, right, preferred_element_type=jnp.float32)
+
+
+def one_hot_blocks(row, blocks):
+    places = lax.broadcasted_iota(jnp.int32, (LANES, LANES), 0)
+    places = places.astype(jnp.float32).astype(jnp.bfloat16)
+    pieces = []
+    for m in range(blocks):
+        wanted = jnp.broadcast_to(row - float(LANES * m), (LANES, LANES)).astype(jnp.bfloat16)
+        one, zero = jnp.ones((), jnp.bfloat16), jnp.zeros((), jnp.bfloat16)
+        pieces.append(jnp.where(places == wanted, one, zero))
+    return jnp.concatenate(pieces, axis=0)
+
+
+def operator_copy(ops_ref, stage, arrived, part):
+    coeffs = ops_ref.shape[0]
+    count = min(8, coeffs - 8 * part)
+    return pltpu.make_async_copy(
+        ops_ref.at[:, pl.ds(8 * part, count), :],
+        stage.at[part, :, pl.ds(0, count), :],
+        arrived.at[part],
+    )
+
+
 def interact_kernel(
-    coeffs, slots, group, spread, tops, fine_ref, tops_ref, upward_ref, fine_list, coarse_list,
-    ops_ref, out_ref,
-    fine_table, coarse_table, fine_picked, coarse_picked, held,
+    spread, tops, fine_ref, tops_ref, upward_ref, fine_list, coarse_list, ops_ref, out_ref,
+    stage, fine_table, coarse_table, fine_picked, coarse_picked, lists, held, arrived,
 ):
     rows = fine_ref.shape[0]
+    coeffs, _, slots = ops_ref.shape
     depth = fine_list.shape[0]
-    step = pl.program_id(0)
-
-    @pl.when(step == 0)
-    def _():
-        ops_high, ops_low = split_upward(upward_ref, held)
-        width = coarse_table.shape[1]
-
-        def shifted(value, amount):
-            extra = width - value.shape[1]
-            if extra:
-                filler = jnp.zeros((rows, extra), jnp.float32)
-                value = jnp.concatenate([value, filler], axis=1)
-            return pltpu.roll(value, amount, 1) if amount else value
-
-        top_moments = jnp.transpose(tops_ref[...])[:rows]
-        coarse = shifted(raise_level(fine_ref[...], ops_high, ops_low), 0)
-        coarse += shifted(top_moments, spread)
-        coarse += shifted(raise_level(top_moments, ops_high, ops_low), spread + tops)
-        for source, table in ((fine_ref[...], fine_table), (coarse, coarse_table)):
-            high, low = halves(source)
-            table[...] = jnp.concatenate([high, low], axis=0)
-
-        def pick(batch, carry):
-            base = pl.multiple_of(8 * batch, 8)
-            for table, entries, picked in (
-                (fine_table, fine_list, fine_picked),
-                (coarse_table, coarse_list, coarse_picked),
-            ):
-                columns = []
-                for k in range(0, 8, 2):
-                    chosen = jnp.concatenate(
-                        [
-                            one_hot(entries[pl.ds(base + k + m, 1), :], table.shape[1])
-                            for m in range(2)
-                        ],
-                        axis=1,
-                    )
-                    both = jnp.dot(table[...], chosen, preferred_element_type=jnp.float32)
-                    value = both[:rows] + both[rows:]
-                    columns += [value[:, :LANES], value[:, LANES:]]
-                picked[:, pl.ds(base, 8), :] = jnp.swapaxes(jnp.stack(columns), 0, 1)
-            return carry
-
-        lax.fori_loop(0, depth // 8, pick, 0)
-        out_ref[...] = jnp.zeros_like(out_ref)
-
-    lane = lax.broadcasted_iota(jnp.int32, (rows, LANES), 1)
-    filler = jnp.zeros((LANES - depth, 2 * LANES), jnp.bfloat16)
-    for part in range(group // 8):
-        block = jnp.swapaxes(ops_ref[:, 8 * part : 8 * part + 8, :], 0, 1)
+    width = coarse_table.shape[1] // 2
+    stride = fine_picked.shape[0] // rows
+    parts = stage.shape[0]
+    for part in range(parts):
+        operator_copy(ops_ref, stage, arrived, part).start()
+
+    ops_high, ops_low = split_upward(upward_ref, held)
+
+    def shifted(value, amount):
+        extra = width - value.shape[1]
+        if extra:
+            filler = jnp.zeros((rows, extra), jnp.float32)
+            value = jnp.concatenate([value, filler], axis=1)
+        return pltpu.roll(value, amount, 1) if amount else value
+
+    top_moments = jnp.transpose(tops_ref[...])[:rows]
+    coarse = shifted(raise_level(fine_ref[...], ops_high, ops_low), 0)
+    coarse += shifted(top_moments, spread)
+    coarse += shifted(raise_level(top_moments, ops_high, ops_low), spread + tops)
+    coarse_table[...] = jnp.concatenate(halves(coarse), axis=1)
+    high, low = halves(fine_ref[...])
+    fine_table[0] = high[:, : 2 * LANES]
+    fine_table[1] = low[:, : 2 * LANES]
+    fine_table[2] = jnp.concatenate([high[:, 2 * LANES :], low[:, 2 * LANES :]], axis=1)
+    lists[0] = fine_list[...].astype(jnp.float32)
+    lists[1] = coarse_list[...].astype(jnp.float32)
+
+    for slot in range(0, depth, 2):
+        pair = [one_hot_blocks(lists[0, slot + m : slot + m + 1, :], 3) for m in range(2)]
+        chosen = jnp.concatenate(pair, axis=1)
+        near, far = chosen[: 2 * LANES], chosen[2 * LANES :]
+        value = matmul(fine_table[0], near) + matmul(fine_table[1], near)
+        value += matmul(fine_table[2], jnp.concatenate([far, far], axis=0))
+        pair = [
+            one_hot_blocks(lists[1, slot + m : slot + m + 1, :], width // LANES) for m in range(2)
+        ]
+        chosen = jnp.concatenate(pair, axis=1)
+        coarse_value = matmul(coarse_table[...], jnp.concatenate([chosen, chosen], axis=0))
+        for m in range(2):
+            columns = slice(m * LANES, (m + 1) * LANES)
+            fine_picked[pl.ds(slot + m, rows, stride), :] = value[:, columns]
+            coarse_picked[pl.ds(slot + m, rows, stride), :] = coarse_value[:, columns]
+
+    for part in range(parts):
+        operator_copy(ops_ref, stage, arrived, part).wait()
+    below = jnp.zeros((LANES - depth, 2 * LANES), jnp.bfloat16)
+    beside = jnp.zeros((coeffs, LANES - slots), jnp.float32)
+    under = jnp.zeros((rows - coeffs, LANES), jnp.float32)
+    total = None
+    for first in range(0, coeffs, 24):
         left = []
         right = []
-        for k in range(8):
-            term = step * group + 8 * part + k
-            op = jnp.where((lane < slots) & (term < coeffs), block[k], 0.0)
+        for term in range(first, min(first + 24, coeffs)):
+            block = stage.at[term // 8].reshape(coeffs * 8, slots)
+            op = block[pl.ds(term % 8, coeffs, 8), :]
+            op = jnp.concatenate([jnp.concatenate([op, beside], axis=1), under], axis=0)
             op_high, op_low = halves(op)
-            data = jnp.concatenate([fine_picked[term], coarse_picked[term]], axis=1)
+            place = pl.ds(term * stride, depth)
+            data = jnp.concatenate([fine_picked[place, :], coarse_picked[place, :]], axis=1)
             high, low = halves(data)
-            high = jnp.concatenate([high, filler], axis=0)
-            low = jnp.concatenate([low, filler], axis=0)
+            high = jnp.concatenate([high, below], axis=0)
+            low = jnp.concatenate([low, below], axis=0)
             left += [op_high, op_high, op_low]
             right += [high, low, high]
-        out_ref[...] += jnp.dot(
-            jnp.concatenate(left, axis=1),
-            jnp.concatenate(right, axis=0),
-            preferred_element_type=jnp.float32,
-        )
+        product = matmul(jnp.concatenate(left, axis=1), jnp.concatenate(right, axis=0))
+        total = product if total is None else total + product
+    out_ref[...] = total
 
 
 def interact(fine, tops_rows, upward_ops, fine_list, coarse_list, ops, spread, tops, coarse_width):
     coeffs, _, slots = ops.shape
     rows, width = fine.shape
     depth = fine_list.shape[0]
-    group = 24
-    whole = lambda array: pl.BlockSpec(array.shape, lambda i: (0, 0))
+    stride = depth + 8
+    parts = round_up(coeffs, 8) // 8
+    vmem = pl.BlockSpec(memory_space=pltpu.VMEM)
     return pl.pallas_call(
-        functools.partial(interact_kernel, coeffs, slots, group, spread, tops),
-        grid=(rows // group,),
-        in_specs=[
-            whole(fine),
-            whole(tops_rows),
-            pl.BlockSpec((coeffs, 8, coeffs), lambda i: (0, 0, 0)),
-            whole(fine_list),
-            whole(coarse_list),
-            pl.BlockSpec((rows, group, LANES), lambda i: (0, i, 0)),
-        ],
-        out_specs=pl.BlockSpec((rows, 2 * LANES), lambda i: (0, 0)),
+        functools.partial(interact_kernel, spread, tops),
+        in_specs=[vmem] * 5 + [pl.BlockSpec(memory_space=pl.ANY)],
+        out_specs=vmem,
         out_shape=jax.ShapeDtypeStruct((rows, 2 * LANES), jnp.float32),
         scratch_shapes=[
-            pltpu.VMEM((2 * rows, width), jnp.bfloat16),
-            pltpu.VMEM((2 * rows, coarse_width), jnp.bfloat16),
-            pltpu.VMEM((rows, depth, LANES), jnp.float32),
-            pltpu.VMEM((rows, depth, LANES), jnp.float32),
+            pltpu.VMEM((parts, coeffs, 8, slots), jnp.float32),
+            pltpu.VMEM((3, rows, 2 * LANES), jnp.bfloat16),
+            pltpu.VMEM((rows, 2 * coarse_width), jnp.bfloat16),
+            pltpu.VMEM((rows * stride, LANES), jnp.float32),
+            pltpu.VMEM((rows * stride, LANES), jnp.float32),
+            pltpu.VMEM((2, depth, LANES), jnp.float32),
             pltpu.VMEM((rows, 8, 2 * LANES), jnp.float32),
+            pltpu.SemaphoreType.DMA((parts,)),
         ],
-        compiler_params=pltpu.CompilerParams(vmem_limit_bytes=48 * 1024 * 1024),
+        compiler_params=pltpu.CompilerParams(vmem_limit_bytes=52 * 1024 * 1024),
         cost_estimate=pl.CostEstimate(
             flops=6 * rows * rows * LANES * 2 * LANES,
             bytes_accessed=4 * rows * rows * LANES,

time: 62.2 us -> 66.1 us (1.063)
  Pallas kernels: 38.9 us -> 43 us
    pallas_call x1, Pallas kernels: 24.3 us -> 28.1 us  [interact(): pl.pallas_call(functools.partial(interact_kernel, spread, tops), in_specs...]
where the time goes in v1:
time: 66.1 us; the launch traced here: 65.7 us
  Pallas kernels  43 us (65%)
  waiting for transfers between devices  8.32 us (13%)
  local copies, waits for them, and re-layouts  5.58 us (8%)
  starting transfers between devices  3.63 us (5%)
  matrix products  3.26 us (5%)
  other arithmetic  1.19 us (2%)
  between operations  0.78 us (1%)
    pallas_call x1, Pallas kernels, interact(): pl.pallas_call(functools.partial(interact_kernel, spread, tops), in_specs...  28.1 us
    pallas_call x1, Pallas kernels, exchange(): pl.pallas_call(functools.partial(exchange_kernel, domains, subs, counts),...  12.3 us
    ppermute x2, waiting for transfers between devices, settle(): moving = lax.ppermute(moving, 'sub', ring)  8.32 us
    unnamed x23, local copies, waits for them, and re-layouts  5.11 us
    ppermute x2, starting transfers between devices, settle(): moving = lax.ppermute(moving, 'sub', ring)  3.63 us
    dot_general x2, matrix products, downward(): jnp.einsum('oab,bp->apo', downward_ops, expansions, precision=precise)  3.26 us
    pallas_call x1, Pallas kernels, evaluate(): pl.pallas_call(potential_kernel, out_shape=jax.ShapeDtypeStruct((1, leave...  2.54 us
  transfers between devices with their start and end apart: 2, of which 2 were waited for; matrix products, arithmetic and copies ran while one was open for 0% of the time, Pallas kernels for 0%

profile of v1, /device:TPU:0, one launch (start us, length us, event | category | flops | bytes accessed | tf_op | source)
XLA Modules:
  0.0 65.7 jit_solution(2837030566541233022)
XLA Ops:
  0.6 0.9 %copy.58 = f32[1,165,128]{2,1,0:T(8,128)S(1)} copy(f32[1,165,128]{2,0,1:T(1,128)} %param.11) | data formatting | bytes 168960
  1.5 3.0 %collective-permute-start = (f32[165,128]{1,0:T(8,128)S(1)}, f32[165,128]{1,0:T(8,128)S(1)}, u32[]{:S(2)}, u32[]{:S(2)}) collective-permute-start(f32[165,128]{1,0:T(8,128)S(1)} %bitcast.41), channel_id=1, source_target_pairs={{0,1},{1,0},{2,3},{3,2},{4,5},{5,4},{6,7},{7,6},{8,9},{9,8},{10,11... | collective-permute-start | bytes 253448 | tf_op jit(solution)/shard_map/ppermute | solution.py:398
  4.5 2.5 %collective-permute-done = f32[165,128]{1,0:T(8,128)S(1)} collective-permute-done((f32[165,128]{1,0:T(8,128)S(1)}, f32[165,128]{1,0:T(8,128)S(1)}, u32[]{:S(2)}, u32[]{:S(2)}) %collective-permute-start) | collective-permute-done | bytes 84512 | tf_op jit(solution)/shard_map/ppermute | solution.py:398
  7.0 0.9 %fusion.17.block_ref = f32[165,128]{1,0:T(8,128)S(1)} fusion(f32[165,128]{1,0:T(8,128)S(1)} %collective-permute-done, f32[1,165,128]{2,0,1:T(1,128)} %param.11), kind=kLoop, calls=%fused_computation.20 | loop fusion | flops 21120 | bytes 253440 | tf_op jit(solution)/shard_map/add | solution.py:399
  7.9 0.0 copy-start
  7.9 1.3 %copy-done = f32[8,165,165]{2,0,1:T(8,128)S(1)} copy-done((f32[8,165,165]{2,0,1:T(8,128)S(1)}, f32[8,165,165]{2,0,1:T(8,128)}, u32[]{:S(2)}) %copy-start) | copy-done | bytes 871224
  9.3 0.0 copy-start.3
  9.3 0.8 %copy-done.3 = s32[94,128]{1,0:T(8,128)S(1)} copy-done((s32[94,128]{1,0:T(8,128)S(1)}, s32[94,128]{1,0:T(8,128)}, u32[]{:S(2)}) %copy-start.3) | copy-done | bytes 48152
  10.1 0.0 copy-start.5
  10.1 0.7 %copy-done.5 = s32[94,16]{0,1:T(8,128)S(1)} copy-done((s32[94,16]{0,1:T(8,128)S(1)}, s32[94,16]{0,1:T(8,128)}, u32[]{:S(2)}) %copy-start.5) | copy-done | bytes 6040
  10.8 0.0 copy-start.6
  10.8 0.7 %copy-done.6 = s32[94,4]{0,1:T(4,128)S(1)} copy-done((s32[94,4]{0,1:T(4,128)S(1)}, s32[94,4]{0,1:T(4,128)}, u32[]{:S(2)}) %copy-start.6) | copy-done | bytes 1528
  11.4 0.0 copy-start.7
  11.4 0.7 %copy-done.7 = s32[94,2]{0,1:T(2,128)S(1)} copy-done((s32[94,2]{0,1:T(2,128)S(1)}, s32[94,2]{0,1:T(2,128)}, u32[]{:S(2)}) %copy-start.7) | copy-done | bytes 776
  12.1 0.0 copy-start.1
  12.1 12.3 %shard_map.122 = (f32[168,384]{1,0:T(8,128)S(1)}, f32[128,256]{1,0:T(8,128)S(1)}, s32[96,128]{1,0:T(8,128)S(1)}, s32[96,128]{1,0:T(8,128)S(1)}) custom-call(f32[165,128]{1,0:T(8,128)S(1)} %fusion.17.block_ref, f32[165,128]{1,0:T(8,128)S(1)} %bitcast.42, f32[165,8,165]{2,1,0:T(8,128)S(1)} %bitcast.39, s32[94,128]{1,0:T(8,128)S(1)} %copy-done.3, ...), custom_call_target="tpu_custom_call" | custom-call | tf_op jit(solution)/shard_map/pallas_call | solution.py:352
  24.4 0.0 copy-done.1
  24.4 0.0 copy-start.10
  24.4 0.0 copy-start.8
  24.4 28.1 %shard_map.123 = f32[168,256]{1,0:T(8,128)S(1)} custom-call(f32[168,384]{1,0:T(8,128)S(1)} %get-tuple-element.6.fine_ref, f32[128,256]{1,0:T(8,128)S(1)} %get-tuple-element.7.tops_ref, f32[165,8,165]{2,1,0:T(8,128)S(1)} %bitcast.40, s32[96,128]{1,0:T(8,128)S(1)} %get-tuple-element.8.fine_list, s32[96,128]{1,0:T(8,128)S(1)} %get-tuple-element.9.coarse_list, ...), custom_call_target="tpu_custom_call" | custom-call | flops 5549064192 | bytes 14450688 | tf_op jit(solution)/shard_map/pallas_call | solution.py:149
  52.6 0.7 %collective-permute-start.1 = (f32[168,256]{1,0:T(8,128)S(1)}, f32[168,256]{1,0:T(8,128)S(1)}, u32[]{:S(2)}, u32[]{:S(2)}) collective-permute-start(f32[168,256]{1,0:T(8,128)S(1)} %shard_map.123), channel_id=1, source_target_pairs={{0,1},{1,0},{2,3},{3,2},{4,5},{5,4},{6,7},{7,6},{8,9},{9,8},{10,11... | collective-permute-start | bytes 516104 | tf_op jit(solution)/shard_map/ppermute | solution.py:398
  53.2 0.0 copy-done.10
  53.2 5.8 %collective-permute-done.1 = f32[168,256]{1,0:T(8,128)S(1)} collective-permute-done((f32[168,256]{1,0:T(8,128)S(1)}, f32[168,256]{1,0:T(8,128)S(1)}, u32[]{:S(2)}, u32[]{:S(2)}) %collective-permute-start.1) | collective-permute-done | bytes 172064 | tf_op jit(solution)/shard_map/ppermute | solution.py:398
  59.1 0.2 slice_reduce_fusion
  59.2 0.0 copy-done.8
  59.3 0.3 multiply_reduce_fusion
  59.5 1.7 %fusion.7 = f32[165,2,8]{0,1,2:T(2,128)S(1)} fusion(f32[8,165,165]{2,0,1:T(8,128)S(1)} %copy-done.8, f32[168,256]{1,0:T(8,128)S(1)} %add.27, f32[8,165]{0,1:T(8,128)S(1)} %multiply_reduce_fusion, s32[]{:T(128)S(6)} %select_n.11), kind=kOutput, calls=%fused_computation.6 | convolution fusion | flops 5227530 | bytes 1534276 | tf_op jit(solution)/shard_map/oab,bp->apo/dot_general | solution.py:389
  61.2 0.0 copy-start.2
  61.2 0.0 copy-start.4
  61.2 0.1 copy.30
  61.3 1.6 %fusion.4 = f32[165,16,8]{0,1,2:T(8,128)S(1)} fusion(f32[8,165,165]{2,0,1:T(8,128)S(1)} %copy-done.8, f32[165,16]{1,0:T(8,128)S(1)} %copy.30, f32[168,256]{1,0:T(8,128)S(1)} %add.27), kind=kOutput, calls=%fused_computation.5 | convolution fusion | flops 41820240 | bytes 1608192 | tf_op jit(solution)/shard_map/oab,bp->apo/dot_general | solution.py:389
  62.9 0.1 copy.57
  63.0 0.1 copy.34
  63.1 0.0 copy-start.9
  63.1 0.0 copy-done.2
  63.2 0.0 copy-done.4
  63.2 2.5 %shard_map.124 = f32[1,2048]{1,0:T(1,128)} custom-call(f32[168,128]{1,0:T(8,128)S(1)} %pad.8.local_ref, s32[1,2048]{1,0:T(1,128)S(1)} %bitcast.43, f32[3,2048]{1,0:T(4,128)S(1)} %copy-done.4, s32[168,128]{1,0:T(8,128)S(1)} %copy-done.2), custom_call_target="tpu_custom_call" | custom-call | tf_op jit(solution)/shard_map/pallas_call | solution.py:199
  65.7 0.0 copy-done.9
  (5 shorter events, 0.1 us)
Async XLA Ops:
  1.5 5.5 %collective-permute-start = (f32[165,128]{1,0:T(8,128)S(1)}, f32[165,128]{1,0:T(8,128)S(1)}, u32[]{:S(2)}, u32[]{:S(2)}) collective-permute-start(f32[165,128]{1,0:T(8,128)S(1)} %bitcast.41), channel_id=1, source_target_pairs={{0,1},{1,0},{2,3},{3,2},{4,5},{5,4},{6,7},{7,6},{8,9},{9,8},{10,11... | collective-permute-start | bytes 253448 | tf_op jit(solution)/shard_map/ppermute | solution.py:398
  7.9 1.3 %copy-start = (f32[8,165,165]{2,0,1:T(8,128)S(1)}, f32[8,165,165]{2,0,1:T(8,128)}, u32[]{:S(2)}) copy-start(f32[8,165,165]{2,0,1:T(8,128)} %param.12) | copy-start | bytes 2613604
  9.3 0.8 %copy-start.3 = (s32[94,128]{1,0:T(8,128)S(1)}, s32[94,128]{1,0:T(8,128)}, u32[]{:S(2)}) copy-start(s32[94,128]{1,0:T(8,128)} %fine_ref.1) | copy-start | bytes 144388
  10.1 0.7 %copy-start.5 = (s32[94,16]{0,1:T(8,128)S(1)}, s32[94,16]{0,1:T(8,128)}, u32[]{:S(2)}) copy-start(s32[94,16]{0,1:T(8,128)} %param.16) | copy-start | bytes 18052
  10.8 0.7 %copy-start.6 = (s32[94,4]{0,1:T(4,128)S(1)}, s32[94,4]{0,1:T(4,128)}, u32[]{:S(2)}) copy-start(s32[94,4]{0,1:T(4,128)} %param.18) | copy-start | bytes 4516
  11.4 0.7 %copy-start.7 = (s32[94,2]{0,1:T(2,128)S(1)}, s32[94,2]{0,1:T(2,128)}, u32[]{:S(2)}) copy-start(s32[94,2]{0,1:T(2,128)} %param.17) | copy-start | bytes 2260
  12.1 12.3 %copy-start.1 = (f32[8,165,165]{2,0,1:T(8,128)S(1)}, f32[8,165,165]{2,0,1:T(8,128)}, u32[]{:S(2)}) copy-start(f32[8,165,165]{2,0,1:T(8,128)} %param.12) | copy-start | bytes 2613604
  24.4 28.8 %copy-start.10 = (s32[2048]{0:T(1024)S(1)}, s32[2048]{0:T(1024)}, u32[]{:S(2)}) copy-start(s32[2048]{0:T(1024)} %param.20) | copy-start | bytes 24580
  24.4 34.8 %copy-start.8 = (f32[8,165,165]{2,0,1:T(8,128)S(1)}, f32[8,165,165]{2,0,1:T(8,128)}, u32[]{:S(2)}) copy-start(f32[8,165,165]{2,0,1:T(8,128)} %param.14) | copy-start | bytes 2613604
  52.6 6.5 %collective-permute-start.1 = (f32[168,256]{1,0:T(8,128)S(1)}, f32[168,256]{1,0:T(8,128)S(1)}, u32[]{:S(2)}, u32[]{:S(2)}) collective-permute-start(f32[168,256]{1,0:T(8,128)S(1)} %shard_map.123), channel_id=1, source_target_pairs={{0,1},{1,0},{2,3},{3,2},{4,5},{5,4},{6,7},{7,6},{8,9},{9,8},{10,11... | collective-permute-start | bytes 516104 | tf_op jit(solution)/shard_map/ppermute | solution.py:398
  61.2 2.0 %copy-start.2 = (s32[168,128]{1,0:T(8,128)S(1)}, s32[168,128]{1,0:T(8,128)}, u32[]{:S(2)}) copy-start(s32[168,128]{1,0:T(8,128)} %constant.36.exponent_ref) | copy-start | bytes 258052
  61.2 2.0 %copy-start.4 = (f32[3,2048]{1,0:T(4,128)S(1)}, f32[3,2048]{1,0:T(4,128)}, u32[]{:S(2)}) copy-start(f32[3,2048]{1,0:T(4,128)} %position_ref.1) | copy-start | bytes 73732
  63.1 2.6 %copy-start.9 = (f32[165,128]{1,0:T(8,128)}, f32[165,128]{1,0:T(8,128)S(1)}, u32[]{:S(2)}) copy-start(f32[165,128]{1,0:T(8,128)S(1)} %slice_add_fusion.2) | copy-start | bytes 253444

commit v2 on v1

v2 whole, which is shorter than its diff:
```python
import functools

import jax
import jax.numpy as jnp
from jax import lax
from jax.experimental import pallas as pl
from jax.experimental.pallas import tpu as pltpu
from jax.sharding import PartitionSpec as P

ORDER = 8
LANES = 128


def round_up(count, unit):
    return -(-count // unit) * unit


def exponents():
    entries = []
    for degree in range(ORDER + 1):
        for along_x in range(degree, -1, -1):
            for along_y in range(degree - along_x, -1, -1):
                entries.append((along_x, along_y, degree - along_x - along_y))
    return entries


def halves(value):
    high = value.astype(jnp.bfloat16)
    low = (value - high.astype(jnp.float32)).astype(jnp.bfloat16)
    return high, low


def one_hot(row, count):
    places = lax.broadcasted_iota(jnp.int32, (count, row.shape[1]), 0)
    return jnp.where(places == row, 1.0, 0.0).astype(jnp.bfloat16)


def matmul(left, right):
    return jnp.dot(left, right, preferred_element_type=jnp.float32)


def one_hot_blocks(row, blocks):
    places = lax.broadcasted_iota(jnp.int32, (LANES, LANES), 0)
    places = places.astype(jnp.float32).astype(jnp.bfloat16)
    pieces = []
    for m in range(blocks):
        wanted = jnp.broadcast_to(row - float(LANES * m), (LANES, LANES)).astype(jnp.bfloat16)
        one, zero = jnp.ones((), jnp.bfloat16), jnp.zeros((), jnp.bfloat16)
        pieces.append(jnp.where(places == wanted, one, zero))
    return jnp.concatenate(pieces, axis=0)


def operator_copy(ops_ref, stage, arrived, part):
    coeffs = ops_ref.shape[0]
    count = min(8, coeffs - 8 * part)
    return pltpu.make_async_copy(
        ops_ref.at[:, pl.ds(8 * part, count), :],
        stage.at[part, :, pl.ds(0, count), :],
        arrived.at[part],
    )


def raise_level(moments, ops_high, ops_low):
    rows, width = moments.shape
    parents = round_up(width // 8, LANES)
    high, low = halves(moments)
    source = lax.broadcasted_iota(jnp.int32, (width, 8 * parents), 0)
    target = lax.broadcasted_iota(jnp.int32, (width, 8 * parents), 1)
    wanted = 8 * (target % parents) + target // parents
    chosen = jnp.where(source == wanted, 1.0, 0.0).astype(jnp.bfloat16)
    both = matmul(jnp.concatenate([high, low], axis=0), chosen)
    filler = jnp.zeros((2 * LANES - rows, parents), jnp.float32)
    stacks = []
    for first in (0, rows):
        pieces = []
        for o in range(8):
            pieces += [both[first : first + rows, o * parents : (o + 1) * parents], filler]
        stacks.append(jnp.concatenate(pieces, axis=0).astype(jnp.bfloat16))
    value = matmul(ops_high[...], stacks[0]) + matmul(ops_high[...], stacks[1])
    return value + matmul(ops_low[...], stacks[0])


def transfer(source, target, sems, index, place):
    return pltpu.make_async_remote_copy(
        src_ref=source,
        dst_ref=target,
        send_sem=sems[0].at[index],
        recv_sem=sems[1].at[index],
        device_id=place,
        device_id_type=pl.DeviceIdType.MESH,
    )


def total_of(first, others):
    for k in range(others.shape[0]):
        first = first + others[k]
    return first


def padded(value, height, width):
    below, beside = height - value.shape[0], width - value.shape[1]
    if beside:
        filler = jnp.zeros((value.shape[0], beside), value.dtype)
        value = jnp.concatenate([value, filler], axis=1)
    if below:
        value = jnp.concatenate([value, jnp.zeros((below, width), value.dtype)], axis=0)
    return value


def fill_octant(ops, octant, high_ref, low_ref):
    coeffs = ops.shape[1]
    at = 2 * LANES * octant
    high_ref[:coeffs, at : at + coeffs], low_ref[:coeffs, at : at + coeffs] = halves(ops[octant])


def spread_level(expansions, offset, ops_high, ops_low):
    rows = expansions.shape[0]
    parent = lax.broadcasted_iota(jnp.int32, (LANES, LANES), 0)
    child = lax.broadcasted_iota(jnp.int32, (LANES, LANES), 1) + offset
    copied = jnp.where(child // 8 == parent, 1.0, 0.0).astype(jnp.bfloat16)
    high, low = halves(expansions)
    both = matmul(jnp.concatenate([high, low], axis=0), copied).astype(jnp.bfloat16)
    wide = jnp.concatenate([both[:rows], both[rows:]], axis=1).astype(jnp.float32)
    wide = padded(wide, 2 * LANES, 2 * LANES)
    octant = (lax.broadcasted_iota(jnp.int32, wide.shape, 1) % LANES + offset) % 8
    pieces = [jnp.where(octant == o, wide, 0.0).astype(jnp.bfloat16) for o in range(8)]
    right = jnp.concatenate(pieces, axis=0)
    first = matmul(ops_high[...], right)
    second = matmul(ops_low[...], right[:, :LANES])
    return first[:, :LANES] + first[:, LANES:] + second


def pick_slots(lists, which, table, picked, rows, blocks):
    depth = lists.shape[1]
    stride = picked.shape[0] // (rows + 1)
    batch = 32 if depth % 32 == 0 else 16

    def step(number, carry):
        base = pl.multiple_of(number * batch, batch)
        for slot in range(0, batch, 2):
            pair = [
                one_hot_blocks(lists[which, pl.ds(base + slot + m, 1), :], blocks)
                for m in range(2)
            ]
            chosen = jnp.concatenate(pair, axis=1)
            if which:
                value = matmul(table[...], jnp.concatenate([chosen, chosen], axis=0))
            else:
                near, far = chosen[: 2 * LANES], chosen[2 * LANES :]
                value = matmul(table[0], near) + matmul(table[1], near)
                value += matmul(table[2], jnp.concatenate([far, far], axis=0))
            for m in range(2):
                at = pl.ds(base + slot + m, rows, stride)
                picked[at, :] = value[:, m * LANES : (m + 1) * LANES]
        return carry

    lax.fori_loop(0, depth // batch, step, 0)


def contract(stage, fine_picked, coarse_picked, rows, depth):
    coeffs, slots = stage.shape[1], stage.shape[3]
    stride = fine_picked.shape[0] // (rows + 1)
    below = jnp.zeros((LANES - depth, 2 * LANES), jnp.bfloat16)
    total = None
    for first in range(0, coeffs, 24):
        left = []
        right = []
        for term in range(first, min(first + 24, coeffs)):
            block = stage.at[term // 8].reshape(coeffs * 8, slots)
            op_high, op_low = halves(padded(block[pl.ds(term % 8, coeffs, 8), :], rows, LANES))
            place = pl.ds(term * stride, depth)
            data = jnp.concatenate([fine_picked[place, :], coarse_picked[place, :]], axis=1)
            high, low = halves(data)
            high = jnp.concatenate([high, below], axis=0)
            low = jnp.concatenate([low, below], axis=0)
            left += [op_high, op_high, op_low]
            right += [high, low, high]
        product = matmul(jnp.concatenate(left, axis=1), jnp.concatenate(right, axis=0))
        total = product if total is None else total + product
    return total


def step_kernel(
    domains, subs, counts, partial_ref, upward_ref, ops_ref, downward_ref, fine_ref, mid_ref,
    top_list_ref, upper_ref, leaf_ref, position_ref, exponent_ref,
    local_out, potential_out,
    mine, upward, downward, fine_in, mid_in, top_in, upper_in, leaves, positions, powers,
    stage, up_high, up_low, down_high, down_low, mids, top_ref, parts, mid_parts, sums,
    mid_sums, low, high, mid_rows, tops, top_rows, lists, turned_lists, fine_table,
    coarse_table, fine_picked, coarse_picked, fine_terms, coarse_terms, fine_parts,
    coarse_parts, chosen_ref, factors_ref,
    load, arrived_ops, part_send, part_recv, side_send, side_recv, top_send, top_recv,
    term_send, term_recv,
):
    domain, sub = lax.axis_index("dom"), lax.axis_index("sub")
    slab, mid, top, spread, all_tops = counts
    count = domains * subs
    flat = domain * subs + sub
    coeffs, cells = mine.shape
    rows = up_high.shape[0]
    depth = lists.shape[1]
    slots = fine_in.shape[0]
    particles = leaves.shape[1]
    width = coarse_table.shape[1] // 2
    part_sems, side_sems = (part_send, part_recv), (side_send, side_recv)
    term_sems = (term_send, term_recv)

    loads = [pltpu.make_async_copy(partial_ref.at[:, 0, :], mine, load.at[0])]
    for o in range(8):
        loads.append(
            pltpu.make_async_copy(upward_ref.at[:, o, :], upward.at[o], load.at[1 + o])
        )
    for k, (source, target) in enumerate(
        (
            (fine_ref, fine_in), (mid_ref, mid_in), (top_list_ref, top_in),
            (upper_ref, upper_in), (leaf_ref, leaves), (position_ref, positions),
            (exponent_ref, powers),
        )
    ):
        loads.append(pltpu.make_async_copy(source, target, load.at[9 + k]))
    downs = [
        pltpu.make_async_copy(downward_ref.at[:, o, :], downward.at[o], load.at[16 + o])
        for o in range(8)
    ]
    for one in loads:
        one.start()
    barrier = pltpu.get_barrier_semaphore()

    def peer(offset):
        place = lax.rem(flat + offset, count)
        return {"dom": place // subs, "sub": lax.rem(place, subs)}

    def greet(offset, carry):
        pl.semaphore_signal(
            barrier, inc=1, device_id=peer(offset), device_id_type=pl.DeviceIdType.MESH
        )
        return carry

    mid_rows[...] = jnp.zeros_like(mid_rows)
    top_rows[...] = jnp.zeros_like(top_rows)
    lax.fori_loop(1, count, greet, 0)
    for ref in (up_high, up_low, down_high, down_low):
        ref[...] = jnp.zeros_like(ref)
    for o in range(8):
        loads[1 + o].wait()
        fill_octant(upward, o, up_high, up_low)
    loads[0].wait()
    for one in downs:
        one.start()
    for part in range(stage.shape[0]):
        operator_copy(ops_ref, stage, arrived_ops, part).start()
    mid_moments = raise_level(padded(mine[...], rows, cells), up_high, up_low)
    top_moments = raise_level(mid_moments, up_high, up_low)
    both = mid_moments + pltpu.roll(top_moments, mid, 1)
    turned = jnp.transpose(padded(both, 2 * LANES, LANES))
    mids[...] = turned[:mid]
    top_ref[...] = turned[mid : mid + top]
    tops[count - 1] = top_ref[...]
    pl.semaphore_wait(barrier, count - 1)

    def send(offset, carry):
        pltpu.make_async_remote_copy(
            src_ref=top_ref,
            dst_ref=tops.at[offset - 1],
            send_sem=top_send,
            recv_sem=top_recv,
            device_id=peer(offset),
            device_id_type=pl.DeviceIdType.MESH,
        ).start()
        return carry

    lax.fori_loop(1, count, send, 0)
    sub_peers = [{"dom": domain, "sub": lax.rem(sub + k + 1, subs)} for k in range(subs - 1)]
    copies = []
    for k, place in enumerate(sub_peers):
        copies.append(transfer(mine, parts.at[k], part_sems, 2 * k, place))
        copies.append(transfer(mids, mid_parts.at[k], part_sems, 2 * k + 1, place))
    for one in copies:
        one.start()

    for one in loads[9:]:
        one.wait()

    def place_in(sources, offset):
        return jnp.where(sources >= 0, sources + offset, -1).astype(jnp.float32)

    lists[0, :slots] = place_in(fine_in[...], slab - domain * slab)
    lists[0, slots:] = jnp.full((depth - slots, LANES), -1.0, jnp.float32)
    turned_lists[...] = jnp.full_like(turned_lists, -1.0)
    start = 0
    for part in (
        place_in(mid_in[...], mid - domain * mid),
        place_in(top_in[...], spread),
        place_in(upper_in[pl.ds(domain * top // 8, 1), :], spread + all_tops),
    ):
        turned_lists[start : start + part.shape[0], :slots] = part
        start += part.shape[0]
    lists[1] = jnp.transpose(turned_lists[...])[:depth]

    for one in copies:
        one.wait()
    sums[...] = total_of(mine[...], parts)
    mid_sums[...] = total_of(mids[...], mid_parts)
    copies = []
    for index, (target, first, move) in enumerate(((low, 0, 1), (high, 2 * mid, domains - 1))):
        place = {"dom": lax.rem(domain + move, domains), "sub": sub}
        copies.append(transfer(sums, target, side_sems, 2 * index, place))
        rows_there = mid_rows.at[pl.ds(first, mid)]
        copies.append(transfer(mid_sums, rows_there, side_sems, 2 * index + 1, place))
    for one in copies:
        one.start()

    def split(block):
        return halves(padded(block, rows, LANES))

    fine_table[0, :, LANES:], fine_table[1, :, LANES:] = split(sums[...])
    for o in range(8):
        downs[o].wait()
        fill_octant(downward, o, down_high, down_low)
    masks = [
        [(powers[:, axis : axis + 1] // bit) % 2 == 1 for bit in (1, 2, 4, 8)]
        for axis in range(3)
    ]

    def factor(number, carry):
        span = pl.ds(pl.multiple_of(number * LANES, LANES), LANES)
        chosen_ref[:, span] = one_hot(leaves[:, span] - domain * slab, cells)
        value = jnp.ones((rows, LANES), jnp.float32)
        for axis in range(3):
            power = positions[axis : axis + 1, span]
            for bit in range(4):
                value = value * jnp.where(masks[axis][bit], power, 1.0)
                power = power * power
        factors_ref[:, span] = value
        return carry

    lax.fori_loop(0, particles // LANES, factor, 0)
    for one in copies:
        one.wait()
    fine_table[0, :, :LANES], fine_table[1, :, :LANES] = split(low[...])
    fine_table[2, :, :LANES], fine_table[2, :, LANES:] = split(high[...])
    pick_slots(lists, 0, fine_table, fine_picked, rows, 3)

    arrived = tops.at[pl.ds(0, count - 1)]
    pltpu.make_async_copy(arrived, arrived, top_recv).wait()

    def gather(offset, carry):
        source = lax.rem(flat + count - offset, count) // subs
        slot = lax.rem(offset + count - 1, count)
        for r in range(top):
            at = pl.ds(source * top + r, 1)
            top_rows[at, :] = top_rows[at, :] + tops[slot, r : r + 1, :]
        return carry

    lax.fori_loop(0, count, gather, 0)

    def shifted(value, amount):
        value = padded(value, rows, width)
        return pltpu.roll(value, amount, 1) if amount else value

    mid_rows[mid : 2 * mid] = mid_sums[...]
    top_moments = jnp.transpose(top_rows[...])[:rows]
    coarse = shifted(top_moments, spread)
    coarse += shifted(raise_level(top_moments, up_high, up_low), spread + all_tops)
    coarse += shifted(jnp.transpose(mid_rows[...])[:rows], 0)
    coarse_table[:, :width], coarse_table[:, width:] = halves(coarse)
    pick_slots(lists, 1, coarse_table, coarse_picked, rows, width // LANES)

    for part in range(stage.shape[0]):
        operator_copy(ops_ref, stage, arrived_ops, part).wait()
    total = contract(stage, fine_picked, coarse_picked, rows, depth)
    fine_terms[...] = total[:, :LANES]
    turned = jnp.transpose(padded(total[:, LANES:], 2 * LANES, LANES))
    coarse_terms[...] = turned[: coarse_terms.shape[0]]
    coarse_copies = []
    fine_copies = []
    for k, place in enumerate(sub_peers):
        coarse_copies.append(
            transfer(coarse_terms, coarse_parts.at[k], term_sems, 2 * k, place)
        )
        fine_copies.append(transfer(fine_terms, fine_parts.at[k], term_sems, 2 * k + 1, place))
    for one in coarse_copies + fine_copies:
        one.start()
    for one in coarse_copies:
        one.wait()
    coarse = jnp.transpose(padded(total_of(coarse_terms[...], coarse_parts), LANES, 2 * LANES))
    coarse = coarse[:rows]
    lane = lax.broadcasted_iota(jnp.int32, coarse.shape, 1)

    def columns(first, number):
        value = pltpu.roll(coarse, LANES - first, 1) if first else coarse
        return jnp.where(lane < number, value, 0.0)

    local = columns(mid + top, 1)
    local = columns(mid, top) + spread_level(local, domain * top % 8, down_high, down_low)
    local = jnp.where(lane < top, local, 0.0)
    local = columns(0, mid) + spread_level(local, 0, down_high, down_low)
    local = spread_level(local, 0, down_high, down_low)
    for one in fine_copies:
        one.wait()
    local = total_of(fine_terms[...], fine_parts) + local
    local_out[...] = local[:coeffs]
    table = jnp.concatenate(halves(local), axis=1)
    for start in range(0, particles, 2 * LANES):
        span = slice(start, start + 2 * LANES)
        chosen = chosen_ref[:, span]
        value = matmul(table, jnp.concatenate([chosen, chosen], axis=0)) * factors_ref[:, span]
        potential_out[:, span] = jnp.sum(value, axis=0, keepdims=True)
    pltpu.make_async_copy(arrived, arrived, top_send).wait()


def shards(
    fine_partial,
    upward_ops,
    interaction_ops,
    downward_ops,
    fine_list,
    mid_list,
    top_list,
    upper_list,
    positions,
    leaf_cell,
):
    domains, subs = lax.axis_size("dom"), lax.axis_size("sub")
    slab = fine_partial.shape[2]
    mid = slab // 8
    top = slab // 64
    slots, coeffs = interaction_ops.shape[:2]
    particles = leaf_cell.shape[0]
    rows = round_up(coeffs, 24)
    depth = round_up(slots, 16)
    parts = round_up(coeffs, 8) // 8
    picked = (rows + 1) * (depth + 8)
    spread = 3 * mid
    tops = top * domains
    coarse_rows = round_up(mid + top + 1, 8)
    counts = (slab, mid, top, spread, tops)
    width = round_up(spread + tops + tops // 8, LANES)
    others = max(subs - 1, 1)
    wide = 2 * LANES
    f32, bf16, i32 = jnp.float32, jnp.bfloat16, jnp.int32
    table = jnp.asarray(exponents(), i32)
    table = jnp.pad(table, ((0, rows - coeffs), (0, LANES - 3)))
    shapes = [
        ((coeffs, slab), f32),
        ((8, coeffs, coeffs), f32),
        ((8, coeffs, coeffs), f32),
        ((slots, slab), i32),
        ((mid, slots), i32),
        ((top, slots), i32),
        ((upper_list.shape[1], slots), i32),
        ((1, particles), i32),
        ((3, particles), f32),
        ((rows, LANES), i32),
        ((parts, coeffs, 8, slots), f32),
        ((rows, 8 * wide), bf16),
        ((rows, 8 * wide), bf16),
        ((rows, 8 * wide), bf16),
        ((rows, 8 * wide), bf16),
        ((mid, wide), f32),
        ((top, wide), f32),
        ((others, coeffs, slab), f32),
        ((others, mid, wide), f32),
        ((coeffs, slab), f32),
        ((mid, wide), f32),
        ((coeffs, slab), f32),
        ((coeffs, slab), f32),
        ((LANES, wide), f32),
        ((domains * subs, top, wide), f32),
        ((round_up(tops, LANES), wide), f32),
        ((2, depth, LANES), f32),
        ((LANES, LANES), f32),
        ((3, rows, wide), bf16),
        ((rows, 2 * width), bf16),
        ((picked, LANES), f32),
        ((picked, LANES), f32),
        ((rows, LANES), f32),
        ((coarse_rows, wide), f32),
        ((others, rows, LANES), f32),
        ((others, coarse_rows, wide), f32),
        ((slab, particles), bf16),
        ((rows, particles), f32),
    ]
    semaphores = [(24,), (parts,)] + 2 * [(2 * others,)] + 2 * [(4,)] + 2 * [()]
    semaphores += 2 * [(2 * others,)]
    vmem = pl.BlockSpec(memory_space=pltpu.VMEM)
    local_fine, potential = pl.pallas_call(
        functools.partial(step_kernel, domains, subs, counts),
        in_specs=[pl.BlockSpec(memory_space=pltpu.HBM)] * 11,
        out_specs=[vmem] * 2,
        out_shape=[
            jax.ShapeDtypeStruct((coeffs, slab), f32),
            jax.ShapeDtypeStruct((1, particles), f32),
        ],
        scratch_shapes=[pltpu.VMEM(*one) for one in shapes]
        + [pltpu.SemaphoreType.DMA(one) if one else pltpu.SemaphoreType.DMA for one in semaphores],
        compiler_params=pltpu.CompilerParams(
            collective_id=0, has_side_effects=True, vmem_limit_bytes=67_043_328
        ),
    )(
        jnp.transpose(fine_partial, (1, 0, 2)),
        jnp.transpose(upward_ops, (1, 0, 2)),
        jnp.transpose(interaction_ops, (1, 2, 0)),
        jnp.transpose(downward_ops, (1, 0, 2)),
        fine_list,
        jnp.transpose(mid_list),
        jnp.transpose(top_list),
        jnp.transpose(upper_list),
        leaf_cell[None],
        positions,
        table,
    )
    return local_fine, potential[0]


def solution(mesh):
    placed = (
        P("sub", None, "dom"),
        P(),
        P("sub", None, None),
        P(),
        P("sub", "dom"),
        P("sub", "dom"),
        P("sub", "dom"),
        P("sub", None),
        P(None, ("dom", "sub")),
        P(("dom", "sub")),
    )
    return jax.shard_map(
        shards,
        mesh=mesh,
        in_specs=placed,
        out_specs=(P(None, "dom"), P(("dom", "sub"))),
        check_vma=False,
    )
```

time: 66.1 us -> 46.2 us (0.70)
  waiting for transfers between devices: 8.32 us -> 0 us
  starting transfers between devices: 3.63 us -> 0 us
  matrix products: 3.26 us -> 0 us
  local copies, waits for them, and re-layouts: 5.58 us -> 2.83 us
  other arithmetic: 1.19 us -> 0 us
    ppermute x2 -> x0, waiting for transfers between devices: 8.32 us -> none  [settle(): moving = lax.ppermute(moving, 'sub', ring)]
    ppermute x2 -> x0, starting transfers between devices: 3.63 us -> none  [settle(): moving = lax.ppermute(moving, 'sub', ring)]
    dot_general x2 -> x0, matrix products: 3.26 us -> none  [downward(): jnp.einsum('oab,bp->apo', downward_ops, expansions, precision=precise)]
    unnamed x23 -> x2, local copies, waits for them, and re-layouts: 5.11 us -> 2.83 us
    add x3 -> x0, other arithmetic: 0.94 us -> none  [the longest x2 0.92 us: settle(): total = total + moving]
    pallas_call x3 -> x1, Pallas kernels: 43 us -> 42.5 us  [shards(): pl.pallas_call(functools.partial(step_kernel, domains, subs, counts), in_...]
  transfers between devices with their start and end apart: 2 -> 0, of which waited for: 2 -> 0; matrix products, arithmetic and copies ran while one was open for 0% -> 0% of each run, Pallas kernels for 0% -> 0%
where the time goes in v2:
time: 46.2 us; the launch traced here: 45.9 us
  Pallas kernels  42.5 us (92%)
  local copies, waits for them, and re-layouts  2.83 us (6%)
  between operations  0.64 us (1%)
    pallas_call x1, Pallas kernels, shards(): pl.pallas_call(functools.partial(step_kernel, domains, subs, counts), in_...  42.5 us
    unnamed x2, local copies, waits for them, and re-layouts  2.83 us

profile of v2, /device:TPU:0, one launch (start us, length us, event | category | flops | bytes accessed | tf_op | source)
XLA Modules:
  0.0 45.9 jit_solution(3385583264308127338)
XLA Ops:
  0.6 42.5 %shard_map.122 = (f32[165,128]{1,0:T(8,128)}, f32[1,2048]{1,0:T(1,128)}) custom-call(f32[165,1,128]{2,1,0:T(1,128)} %bitcast.12, f32[165,8,165]{2,1,0:T(8,128)} %bitcast.10, f32[165,165,94]{2,1,0:T(8,128)} %bitcast.9, f32[165,8,165]{2,1,0:T(8,128)} %bitcast.11, s32[94,128]{1,0:T(8,128)} %fine_ref.1, s32[16,94]{1,0:T(8,128)} %bitcast.13, s32[2,94]{1,0:T(2,128)} %bitcast.17, ...), custom_call_target="tpu_custom_call" | custom-call | tf_op jit(solution)/shard_map/pallas_call | solution.py:487
  43.1 1.5 %copy.15 = f32[165,128]{1,0:T(8,128)} copy(f32[165,128]{1,0:T(8,128)} %get-tuple-element.8) | data formatting | bytes 168960
  44.6 1.3 %copy.16 = f32[2048]{0:T(1024)} copy(f32[2048]{0:T(1024)} %bitcast.15) | data formatting | bytes 16384

commit v3 on v2

--- a/solution.py
+++ b/solution.py
@@ -43,7 +43,7 @@
     places = lax.broadcasted_iota(jnp.int32, (LANES, LANES), 0)
     places = places.astype(jnp.float32).astype(jnp.bfloat16)
     pieces = []
-    for m in range(blocks):
+    for m in blocks:
         wanted = jnp.broadcast_to(row - float(LANES * m), (LANES, LANES)).astype(jnp.bfloat16)
         one, zero = jnp.ones((), jnp.bfloat16), jnp.zeros((), jnp.bfloat16)
         pieces.append(jnp.where(places == wanted, one, zero))
@@ -130,8 +130,8 @@
     return first[:, :LANES] + first[:, LANES:] + second
 
 
-def pick_slots(lists, which, table, picked, rows, blocks):
-    depth = lists.shape[1]
+def pick_slots(list_ref, tables, picked, rows, blocks, repeats, adding):
+    depth = list_ref.shape[0]
     stride = picked.shape[0] // (rows + 1)
     batch = 32 if depth % 32 == 0 else 16
 
@@ -139,19 +139,17 @@
         base = pl.multiple_of(number * batch, batch)
         for slot in range(0, batch, 2):
             pair = [
-                one_hot_blocks(lists[which, pl.ds(base + slot + m, 1), :], blocks)
-                for m in range(2)
+                one_hot_blocks(list_ref[pl.ds(base + slot + m, 1), :], blocks) for m in range(2)
             ]
             chosen = jnp.concatenate(pair, axis=1)
-            if which:
-                value = matmul(table[...], jnp.concatenate([chosen, chosen], axis=0))
-            else:
-                near, far = chosen[: 2 * LANES], chosen[2 * LANES :]
-                value = matmul(table[0], near) + matmul(table[1], near)
-                value += matmul(table[2], jnp.concatenate([far, far], axis=0))
+            chosen = jnp.concatenate([chosen] * repeats, axis=0)
+            value = matmul(tables[0][...], chosen)
+            for table in tables[1:]:
+                value += matmul(table[...], chosen)
             for m in range(2):
                 at = pl.ds(base + slot + m, rows, stride)
-                picked[at, :] = value[:, m * LANES : (m + 1) * LANES]
+                part = value[:, m * LANES : (m + 1) * LANES]
+                picked[at, :] = picked[at, :] + part if adding else part
         return carry
 
     lax.fori_loop(0, depth // batch, step, 0)
@@ -188,7 +186,7 @@
     stage, up_high, up_low, down_high, down_low, mids, top_ref, parts, mid_parts, sums,
     mid_sums, low, high, mid_rows, tops, top_rows, lists, turned_lists, fine_table,
     coarse_table, fine_picked, coarse_picked, fine_terms, coarse_terms, fine_parts,
-    coarse_parts, chosen_ref, factors_ref,
+    coarse_parts, chosen_ref, factors_ref, coarse_ref,
     load, arrived_ops, part_send, part_recv, side_send, side_recv, top_send, top_recv,
     term_send, term_recv,
 ):
@@ -297,6 +295,39 @@
         start += part.shape[0]
     lists[1] = jnp.transpose(turned_lists[...])[:depth]
 
+    lane = lax.broadcasted_iota(jnp.int32, (rows, LANES), 1)
+    takes = []
+    for axis in range(3):
+        taken = (lane < 48) & (lane % 16 == powers[:, axis : axis + 1])
+        takes.append(jnp.where(taken, 1.0, 0.0).astype(jnp.bfloat16))
+    power = lax.broadcasted_iota(jnp.int32, (16, 2 * LANES), 0)
+    power_bits = [(power // bit) % 2 == 1 for bit in (1, 2, 4, 8)]
+    below = jnp.zeros((LANES - 48, 2 * LANES), jnp.bfloat16)
+
+    def factor(number, carry):
+        span = pl.ds(pl.multiple_of(number * 2 * LANES, 2 * LANES), 2 * LANES)
+        chosen_ref[:, span] = one_hot(leaves[:, span] - domain * slab, cells)
+        value = None
+        for axis in range(3):
+            base = positions[axis : axis + 1, span]
+            raised = jnp.ones((16, 2 * LANES), jnp.float32)
+            for bit in power_bits:
+                raised = raised * jnp.where(bit, base, 1.0)
+                base = base * base
+            first, rest = halves(raised)
+            left_over = raised - first.astype(jnp.float32) - rest.astype(jnp.float32)
+            stack = jnp.concatenate(
+                [first, rest, left_over.astype(jnp.bfloat16), below], axis=0
+            )
+            taken = matmul(takes[axis], stack)
+            value = taken if value is None else value * taken
+        factors_ref[:, span] = value
+        return carry
+
+    lax.fori_loop(0, particles // (2 * LANES), factor, 0)
+    for o in range(8):
+        downs[o].wait()
+        fill_octant(downward, o, down_high, down_low)
     for one in copies:
         one.wait()
     sums[...] = total_of(mine[...], parts)
@@ -313,34 +344,8 @@
     def split(block):
         return halves(padded(block, rows, LANES))
 
-    fine_table[0, :, LANES:], fine_table[1, :, LANES:] = split(sums[...])
-    for o in range(8):
-        downs[o].wait()
-        fill_octant(downward, o, down_high, down_low)
-    masks = [
-        [(powers[:, axis : axis + 1] // bit) % 2 == 1 for bit in (1, 2, 4, 8)]
-        for axis in range(3)
-    ]
-
-    def factor(number, carry):
-        span = pl.ds(pl.multiple_of(number * LANES, LANES), LANES)
-        chosen_ref[:, span] = one_hot(leaves[:, span] - domain * slab, cells)
-        value = jnp.ones((rows, LANES), jnp.float32)
-        for axis in range(3):
-            power = positions[axis : axis + 1, span]
-            for bit in range(4):
-                value = value * jnp.where(masks[axis][bit], power, 1.0)
-                power = power * power
-        factors_ref[:, span] = value
-        return carry
-
-    lax.fori_loop(0, particles // LANES, factor, 0)
-    for one in copies:
-        one.wait()
-    fine_table[0, :, :LANES], fine_table[1, :, :LANES] = split(low[...])
-    fine_table[2, :, :LANES], fine_table[2, :, LANES:] = split(high[...])
-    pick_slots(lists, 0, fine_table, fine_picked, rows, 3)
-
+    fine_table[0, :, :LANES], fine_table[0, :, LANES:] = split(sums[...])
+    pick_slots(lists.at[0], [fine_table.at[0]], fine_picked, rows, (1,), 2, False)
     arrived = tops.at[pl.ds(0, count - 1)]
     pltpu.make_async_copy(arrived, arrived, top_recv).wait()
 
@@ -358,13 +363,22 @@
         value = padded(value, rows, width)
         return pltpu.roll(value, amount, 1) if amount else value
 
-    mid_rows[mid : 2 * mid] = mid_sums[...]
     top_moments = jnp.transpose(top_rows[...])[:rows]
     coarse = shifted(top_moments, spread)
     coarse += shifted(raise_level(top_moments, up_high, up_low), spread + all_tops)
-    coarse += shifted(jnp.transpose(mid_rows[...])[:rows], 0)
+    coarse_ref[...] = coarse
+    for one in copies:
+        one.wait()
+    fine_table[1, :, :LANES], fine_table[2, :, :LANES] = split(low[...])
+    fine_table[1, :, LANES:], fine_table[2, :, LANES:] = split(high[...])
+    sides = [fine_table.at[1], fine_table.at[2]]
+    pick_slots(lists.at[0], sides, fine_picked, rows, (0, 2), 1, True)
+
+    mid_rows[mid : 2 * mid] = mid_sums[...]
+    coarse = coarse_ref[...] + shifted(jnp.transpose(mid_rows[...])[:rows], 0)
     coarse_table[:, :width], coarse_table[:, width:] = halves(coarse)
-    pick_slots(lists, 1, coarse_table, coarse_picked, rows, width // LANES)
+    blocks = tuple(range(width // LANES))
+    pick_slots(lists.at[1], [coarse_table], coarse_picked, rows, blocks, 2, False)
 
     for part in range(stage.shape[0]):
         operator_copy(ops_ref, stage, arrived_ops, part).wait()
@@ -480,6 +494,7 @@
         ((others, coarse_rows, wide), f32),
         ((slab, particles), bf16),
         ((rows, particles), f32),
+        ((rows, width), f32),
     ]
     semaphores = [(24,), (parts,)] + 2 * [(2 * others,)] + 2 * [(4,)] + 2 * [()]
     semaphores += 2 * [(2 * others,)]
@@ -510,6 +525,33 @@
         positions,
         table,
     )
+    return deliver(local_fine, potential)
+
+
+def deliver_kernel(local_ref, potential_ref, local_out, potential_out, local, potential, sems):
+    ways = ((local_ref, local, local_out), (potential_ref, potential, potential_out))
+    loads = [pltpu.make_async_copy(way[0], way[1], sems.at[k]) for k, way in enumerate(ways)]
+    stores = [pltpu.make_async_copy(way[1], way[2], sems.at[2 + k]) for k, way in enumerate(ways)]
+    for one in loads:
+        one.start()
+    for load, store in zip(loads, stores):
+        load.wait()
+        store.start()
+    for one in stores:
+        one.wait()
+
+
+def deliver(local_fine, potential):
+    shapes = (local_fine.shape, potential.shape)
+    local_fine, potential = pl.pallas_call(
+        deliver_kernel,
+        in_specs=[pl.BlockSpec(memory_space=pltpu.HBM)] * 2,
+        out_specs=[pl.BlockSpec(memory_space=pltpu.HBM)] * 2,
+        out_shape=[jax.ShapeDtypeStruct(one, jnp.float32) for one in shapes],
+        scratch_shapes=[pltpu.VMEM(one, jnp.float32) for one in shapes]
+        + [pltpu.SemaphoreType.DMA((4,))],
+        compiler_params=pltpu.CompilerParams(vmem_limit_bytes=67_043_328),
+    )(local_fine, potential)
     return local_fine, potential[0]
 
 

time: 46.2 us -> 42.4 us (0.918)
  local copies, waits for them, and re-layouts: 2.83 us -> 0 us
  Pallas kernels: 42.5 us -> 41.4 us
    unnamed x2 -> x0, local copies, waits for them, and re-layouts: 2.83 us -> none
    pallas_call x1, Pallas kernels: 42.5 us -> 39.8 us  [shards(): pl.pallas_call(functools.partial(step_kernel, domains, subs, counts), in_...]
    pallas_call x0 -> x1, Pallas kernels: none -> 1.56 us  [deliver(): pl.pallas_call(deliver_kernel, in_specs=[pl.BlockSpec(memory_space=pltpu....]
where the time goes in v3:
time: 42.4 us; the launch traced here: 42.2 us
  Pallas kernels  41.4 us (98%)
  between operations  0.8 us (2%)
    pallas_call x1, Pallas kernels, shards(): pl.pallas_call(functools.partial(step_kernel, domains, subs, counts), in_...  39.8 us
    pallas_call x1, Pallas kernels, deliver(): pl.pallas_call(deliver_kernel, in_specs=[pl.BlockSpec(memory_space=pltpu....  1.56 us

profile of v3, /device:TPU:0, one launch (start us, length us, event | category | flops | bytes accessed | tf_op | source)
XLA Modules:
  0.0 42.2 jit_solution(505287281137886214)
XLA Ops:
  0.6 39.8 %shard_map.122 = (f32[165,128]{1,0:T(8,128)}, f32[1,2048]{1,0:T(1,128)}) custom-call(f32[165,1,128]{2,1,0:T(1,128)} %bitcast.12, f32[165,8,165]{2,1,0:T(8,128)} %bitcast.10, f32[165,165,94]{2,1,0:T(8,128)} %bitcast.9, f32[165,8,165]{2,1,0:T(8,128)} %bitcast.11, s32[94,128]{1,0:T(8,128)} %fine_ref.1, s32[16,94]{1,0:T(8,128)} %bitcast.13, s32[2,94]{1,0:T(2,128)} %bitcast.16, ...), custom_call_target="tpu_custom_call" | custom-call | tf_op jit(solution)/shard_map/pallas_call | solution.py:502
  40.5 1.6 %shard_map.123 = (f32[165,128]{1,0:T(8,128)}, f32[1,2048]{1,0:T(1,128)}) custom-call(f32[165,128]{1,0:T(8,128)} %get-tuple-element.6.local_ref, f32[1,2048]{1,0:T(1,128)} %get-tuple-element.7.potential_ref), custom_call_target="tpu_custom_call" | custom-call | tf_op jit(solution)/shard_map/pallas_call | solution.py:546

commit v4 on v3

--- a/solution.py
+++ b/solution.py
@@ -267,7 +267,6 @@
         ).start()
         return carry
 
-    lax.fori_loop(1, count, send, 0)
     sub_peers = [{"dom": domain, "sub": lax.rem(sub + k + 1, subs)} for k in range(subs - 1)]
     copies = []
     for k, place in enumerate(sub_peers):
@@ -275,6 +274,7 @@
         copies.append(transfer(mids, mid_parts.at[k], part_sems, 2 * k + 1, place))
     for one in copies:
         one.start()
+    lax.fori_loop(1, count, send, 0)
 
     for one in loads[9:]:
         one.wait()

time: 42.4 us -> 41.9 us (0.988)
  Pallas kernels: 41.4 us -> 40.9 us
    pallas_call x1, Pallas kernels: 39.8 us -> 39.4 us  [shards(): pl.pallas_call(functools.partial(step_kernel, domains, subs, counts), in_...]
where the time goes in v4:
time: 41.9 us; the launch traced here: 41.7 us
  Pallas kernels  40.9 us (98%)
  between operations  0.8 us (2%)
    pallas_call x1, Pallas kernels, shards(): pl.pallas_call(functools.partial(step_kernel, domains, subs, counts), in_...  39.4 us
    pallas_call x1, Pallas kernels, deliver(): pl.pallas_call(deliver_kernel, in_specs=[pl.BlockSpec(memory_space=pltpu....  1.56 us

profile of v4, /device:TPU:0, one launch (start us, length us, event | category | flops | bytes accessed | tf_op | source)
XLA Modules:
  0.0 41.7 jit_solution(15509894781029463649)
XLA Ops:
  0.6 39.4 %shard_map.122 = (f32[165,128]{1,0:T(8,128)}, f32[1,2048]{1,0:T(1,128)}) custom-call(f32[165,1,128]{2,1,0:T(1,128)} %bitcast.12, f32[165,8,165]{2,1,0:T(8,128)} %bitcast.10, f32[165,165,94]{2,1,0:T(8,128)} %bitcast.9, f32[165,8,165]{2,1,0:T(8,128)} %bitcast.11, s32[94,128]{1,0:T(8,128)} %fine_ref.1, s32[16,94]{1,0:T(8,128)} %bitcast.13, s32[2,94]{1,0:T(2,128)} %bitcast.16, ...), custom_call_target="tpu_custom_call" | custom-call | tf_op jit(solution)/shard_map/pallas_call | solution.py:502
  40.0 1.6 %shard_map.123 = (f32[165,128]{1,0:T(8,128)}, f32[1,2048]{1,0:T(1,128)}) custom-call(f32[165,128]{1,0:T(8,128)} %get-tuple-element.6.local_ref, f32[1,2048]{1,0:T(1,128)} %get-tuple-element.7.potential_ref), custom_call_target="tpu_custom_call" | custom-call | tf_op jit(solution)/shard_map/pallas_call | solution.py:546
